TPU v7x, 32 devices: a whole 2x2x4 slice. The times are simulated.
32 devices in a mesh: grp: 2 (over y), vec: 4 (over z), occ: 2 (over x), wlk: 2 (over core).
Axes of the slice: x: 2, y: 2, z: 4, core: 2. Of those that a mesh axis runs over, the one named last changes fastest.
Arguments:
- chol_half: bfloat16 [256, 256, 2048], P(('grp', 'vec'), 'occ'), parts along dimension 0, may hold values from -0.046875 to 0.046875
- theta: bfloat16 [8, 2048, 256], P(('grp', 'wlk'), 'vec', 'occ'), parts along dimension 0, may hold values from -6 to 6
Outputs:
- theta_grad: float32 [8, 2048, 256], P(('grp', 'wlk'), 'vec', 'occ'), parts along dimension 0
There are 2 independent parts, one for each index of `grp`. A program takes and returns all parts, laid end to end along the dimension named above; each array names one. Nothing has to cross between parts.
All inputs are finite; a program needn't handle non-finite values.
Results may differ from a plain program's by a relative error of at most 0.0042.
Values may be sent and summed in bfloat16 or wider, within the bound.
A program may use at most 64 MiB of HBM per device.

v0:
```python
import functools

import jax
import jax.numpy as jnp
from jax import lax
from jax.experimental import pallas as pl
from jax.experimental.pallas import tpu as pltpu
from jax.sharding import PartitionSpec as P

MESH = pl.DeviceIdType.MESH
F32 = jnp.float32
BF16 = jnp.bfloat16


def kernel(nz, dims, chol, theta, out, cv, thp, thd, asend, arecv, adiag, accd, accr, gsend, grecv, gown, xs, xr,
           csem, txs, txr, tzs, tzr, ass, asr, gss, gsr, xss, xsr):
    G, R, M, W, Q, CH = dims
    GC = G // CH
    z = lax.axis_index("vec")
    partner = {"occ": 1 - lax.axis_index("occ")}
    peers = [lax.rem(z + k, nz) for k in range(1, nz)]
    mine = pl.ds(pl.multiple_of(z * Q, Q), Q)

    def c_copy(c):
        part = pl.ds(c * GC, GC)
        return pltpu.make_async_copy(chol.at[part], cv.at[part], csem.at[c])

    def remote(src, dst, ss, rs, to):
        return pltpu.make_async_remote_copy(src_ref=src, dst_ref=dst, send_sem=ss, recv_sem=rs, device_id=to, device_id_type=MESH)

    for c in range(CH):
        c_copy(c).start()

    barrier = pltpu.get_barrier_semaphore()
    pl.semaphore_signal(barrier, inc=1, device_id=partner, device_id_type=MESH)
    for peer in peers:
        pl.semaphore_signal(barrier, inc=1, device_id={"vec": peer}, device_id_type=MESH)
    pl.semaphore_wait(barrier, nz)

    def theta_x(w):
        return remote(theta.at[w], thp.at[w, mine], txs.at[w], txr.at[w], partner)

    def rows_of(s):
        return pl.ds(pl.multiple_of(s * Q, Q), Q)

    def theta_p(w, k, s):
        rows = rows_of(s)
        return remote(thp.at[w, rows], thp.at[w, rows], tzs.at[w, k], tzr.at[w, s], {"vec": peers[k]})

    def theta_d(w, k, s):
        return remote(theta.at[w], thd.at[rows_of(s), pl.ds(w * R, R)], tzs.at[W + w, k], tzr.at[W + w, s], {"vec": peers[k]})

    for w in range(W):
        theta_x(w).start()
    for w in range(W):
        theta_x(w).wait_recv()
        for k in range(nz - 1):
            theta_p(w, k, z).start()
    for w in range(W):
        for k in range(nz - 1):
            theta_d(w, k, z).start()
        thd[mine, pl.ds(w * R, R)] = theta[w]

    def a_copy(w, c):
        part = pl.ds(c * GC, GC)
        return remote(asend.at[w, part], arecv.at[w, part], ass.at[w, c], asr.at[w, c], partner)

    for w in range(W):
        for k in range(nz - 1):
            theta_p(w, k, peers[k]).wait_recv()

        @pl.loop(0, CH)
        def _(c):
            if w == 0:
                c_copy(c).wait()
            part = pl.ds(c * GC, GC)
            block = jnp.dot(cv[part].reshape(GC * R, M), thp[w], preferred_element_type=F32)
            asend[w, part] = block.astype(BF16).reshape(GC, R, R)
            a_copy(w, c).start()

    def g_copy(e, k, s, d):
        return remote(gsend.at[e, d], grecv.at[e, s], gss.at[e, k], gsr.at[e, s], {"vec": peers[k]})

    def scatter(e, acc, first):
        rows = pl.ds(first, R)
        for d in range(nz):
            gsend[e, d] = acc[rows, pl.ds(d * Q, Q)].astype(BF16)
        gown[e] = acc[rows, mine]
        for k in range(nz - 1):
            g_copy(e, k, z, peers[k]).start()

    def gathered(e):
        total = gown[e]
        for k in range(nz - 1):
            g_copy(e, k, peers[k], peers[k]).wait_recv()
            total = total + grecv[e, peers[k]].astype(F32)
        return total

    def x_copy(w):
        return remote(xs.at[w], xr.at[w], xss.at[w], xsr.at[w], partner)

    def add_chunk(acc, lhs, part):
        for n in range(nz):
            cols = pl.ds(n * Q, Q)
            acc[:, cols] += jnp.dot(lhs, cv[part, :, cols].reshape(GC * R, Q), preferred_element_type=F32)

    def received(w):
        accr[...] = jnp.zeros_like(accr)

        @pl.loop(0, CH)
        def _(c):
            a_copy(w, c).wait_recv()
            part = pl.ds(c * GC, GC)
            block = arecv[w, part]
            add_chunk(accr, jnp.concatenate([block[g] for g in range(GC)], axis=1), part)

        scatter(W + w, accr, 0)

    received(0)
    for w in range(W):
        for k in range(nz - 1):
            theta_d(w, k, peers[k]).wait_recv()
    accd[...] = jnp.zeros_like(accd)

    @pl.loop(0, CH)
    def _(c):
        part = pl.ds(c * GC, GC)
        block = jnp.dot(cv[part].reshape(GC * R, M), thd[...], preferred_element_type=F32)
        adiag[part] = block.astype(BF16).reshape(GC, R, W * R)

    @pl.loop(0, CH)
    def _(c):
        part = pl.ds(c * GC, GC)
        block = adiag[part]
        lhs = jnp.concatenate(
            [jnp.concatenate([block[g, :, w * R:(w + 1) * R] for g in range(GC)], axis=1) for w in range(W)], axis=0
        )
        add_chunk(accd, lhs, part)

    for w in range(W):
        scatter(w, accd, w * R)
        if w + 1 < W:
            received(w + 1)

    for w in range(W):
        xs[w] = gathered(W + w).astype(BF16)
        x_copy(w).start()
    for w in range(W):
        gown[w] = gathered(w)
    for w in range(W):
        x_copy(w).wait_recv()
        out[w] = -(gown[w] + xr[w].astype(F32)).T

    for w in range(W):
        theta_x(w).wait_send()
        x_copy(w).wait_send()
        for k in range(nz - 1):
            theta_p(w, k, z).wait_send()
            theta_d(w, k, z).wait_send()
            g_copy(w, k, z, peers[k]).wait_send()
            g_copy(W + w, k, z, peers[k]).wait_send()

        @pl.loop(0, CH)
        def _(c):
            a_copy(w, c).wait_send()


def fused(nz, chol_half, theta):
    G, R, M = chol_half.shape
    W, Q, _ = theta.shape
    CH = 8 if G % 8 == 0 else 1
    dims = (G, R, M, W, Q, CH)
    dma = pltpu.SemaphoreType.DMA
    return pl.pallas_call(
        functools.partial(kernel, nz, dims),
        out_shape=jax.ShapeDtypeStruct((W, Q, R), F32),
        in_specs=[pl.BlockSpec(memory_space=pl.ANY), pl.BlockSpec(memory_space=pltpu.VMEM)],
        out_specs=pl.BlockSpec(memory_space=pltpu.VMEM),
        scratch_shapes=[
            pltpu.VMEM((G, R, M), BF16),
            pltpu.VMEM((W, M, R), BF16),
            pltpu.VMEM((M, W * R), BF16),
            pltpu.VMEM((W, G, R, R), BF16),
            pltpu.VMEM((W, G, R, R), BF16),
            pltpu.VMEM((G, R, W * R), BF16),
            pltpu.VMEM((W * R, M), F32),
            pltpu.VMEM((R, M), F32),
            pltpu.VMEM((2 * W, nz, R, Q), BF16),
            pltpu.VMEM((2 * W, nz, R, Q), BF16),
            pltpu.VMEM((2 * W, R, Q), F32),
            pltpu.VMEM((W, R, Q), BF16),
            pltpu.VMEM((W, R, Q), BF16),
            dma((CH,)),
            dma((W,)),
            dma((W,)),
            dma((2 * W, nz)),
            dma((2 * W, nz)),
            dma((W, CH)),
            dma((W, CH)),
            dma((2 * W, nz)),
            dma((2 * W, nz)),
            dma((W,)),
            dma((W,)),
        ],
        compiler_params=pltpu.CompilerParams(collective_id=0, has_side_effects=True, vmem_limit_bytes=60 << 20),
    )(chol_half, theta)


def on_device(mesh, chol_half, theta):
    G, R, M = chol_half.shape
    nz = mesh.shape["vec"]
    if mesh.shape["occ"] == 2 and R % 128 == 0 and theta.shape[1] % 128 == 0 and G * R * M <= 8 << 20:
        return fused(nz, chol_half, theta)
    widened = lax.all_gather(theta, "occ", axis=2, tiled=True)
    amplitude_sums = jnp.einsum(
        "gip,wpj->wgij", chol_half, lax.all_gather(widened, "vec", axis=1, tiled=True), preferred_element_type=F32
    )
    amplitudes = amplitude_sums.astype(BF16)
    swapped = lax.all_to_all(amplitudes, "occ", split_axis=3, concat_axis=2, tiled=True)
    summed_rows = lax.psum_scatter(
        jnp.einsum("gap,wgba->pwb", chol_half, swapped, preferred_element_type=F32),
        "vec",
        scatter_dimension=0,
        tiled=True,
    )
    owned = lax.psum_scatter(summed_rows, "occ", scatter_dimension=2, tiled=True)
    return -jnp.transpose(owned, (1, 0, 2))


def solution(mesh):
    return jax.shard_map(
        functools.partial(on_device, mesh),
        mesh=mesh,
        in_specs=(P(("grp", "vec"), "occ", None), P(("grp", "wlk"), "vec", "occ")),
        out_specs=P(("grp", "wlk"), "vec", "occ"),
        check_vma=False,
    )
```

profile of v0, /device:TPU:24, one launch (start us, length us, event | category | flops | bytes accessed | tf_op | source)
XLA Modules:
  0.0 107.0 jit_solution(2619808638277667203)
XLA Ops:
  0.0 105.1 %shard_map.28 = f32[2,512,128]{2,1,0:T(8,128)} custom-call(bf16[32,128,2048]{2,1,0:T(8,128)(2,1)} %chol.1, bf16[2,512,128]{2,1,0:T(8,128)(2,1)} %theta.1), custom_call_target="tpu_custom_call" | custom-call | tf_op jit(solution)/shard_map/pallas_call | solution.py:174
  105.2 1.9 %copy.4 = f32[2,512,128]{2,1,0:T(8,128)} copy(f32[2,512,128]{2,1,0:T(8,128)} %shard_map.28) | data formatting | bytes 1048576
where the time goes:
time: 107 us
  Pallas kernels  105 us (98%)
  local copies, waits for them, and re-layouts  1.87 us (2%)
    pallas_call x1, Pallas kernels, fused(): pl.pallas_call(functools.partial(kernel, nz, dims), out_shape=jax.ShapeDt...  105 us

commit v1 on v0

v1 whole, which is shorter than its diff:
```python
import functools

import jax
import jax.numpy as jnp
from jax import lax
from jax.experimental import pallas as pl
from jax.experimental.pallas import tpu as pltpu
from jax.sharding import PartitionSpec as P

MESH = pl.DeviceIdType.MESH
F32 = jnp.float32
BF16 = jnp.bfloat16


def kernel(dims, chol, theta, out, cv, tho, thp, asend, arecv, adiag, acc, gs, gf, gc, gr, gown, xs, xr,
           csem, txs, txr, ags, agr, ass, asr, gss, gsr, xss, xsr):
    G, R, M, W, Q, CH, NQ, pieces, parts = dims
    z = lax.axis_index("vec")
    partner = {"occ": 1 - lax.axis_index("occ")}
    side = z // 2
    near, edge = 1 + side, 3 * side
    far, end = 3 - near, 3 - edge
    inner = z == near
    outer = z == edge
    mate = near + edge - z
    mine = pl.ds(pl.multiple_of(z * Q, Q), Q)
    GC = G // CH
    QC = Q // NQ

    drains = []

    def remote(src, dst, ss, rs, to):
        return pltpu.make_async_remote_copy(src_ref=src, dst_ref=dst, send_sem=ss, recv_sem=rs, device_id=to, device_id_type=MESH)

    def on(s):
        return {"vec": s}

    def c_copy(c):
        part = pl.ds(c * GC, GC)
        return pltpu.make_async_copy(chol.at[part], cv.at[part], csem.at[c])

    for c in range(CH):
        c_copy(c).start()

    barrier = pltpu.get_barrier_semaphore()
    pl.semaphore_signal(barrier, inc=1, device_id=partner, device_id_type=MESH)
    for k in range(1, 4):
        pl.semaphore_signal(barrier, inc=1, device_id=on(lax.rem(z + k, 4)), device_id_type=MESH)
    acc[...] = jnp.zeros_like(acc)
    for w in range(W):
        tho[w, mine] = theta[w]
    pl.semaphore_wait(barrier, 4)

    def rows_of(s, q, n):
        size = Q // n
        return pl.ds(pl.multiple_of(s * Q + q * size, size), size)

    def theta_x(w, q, n, source=None):
        source = z if source is None else source
        rows = rows_of(source, q, n)
        src = theta.at[w, pl.ds(q * (Q // n), Q // n)] if source is z else tho.at[w, rows]
        return remote(src, thp.at[w, rows], txs.at[w, q, source], txr.at[w, q, source], partner)

    def cross(w, q, n, source=None):
        theta_x(w, q, n, source).start()
        drains.append(theta_x(w, q, n, source).wait_send)

    class Gather:
        def __init__(self, s, buf, w, n):
            self.s, self.buf, self.w, self.n = s, buf, w, n

        def copy(self, q, kind, source, to):
            ref = self.buf.at[self.w, rows_of(source, q, self.n)]
            src = theta.at[self.w, pl.ds(q * (Q // self.n), Q // self.n)] if source is z and self.buf is tho else ref
            return remote(src, ref, ags.at[self.s, q, kind], agr.at[self.s, q, source], on(to))

        def start(self, q=0):
            self.copy(q, 0, z, mate).start()
            self.copy(q, 1, z, far).start()
            pl.when(inner)(lambda: self.copy(q, 2, z, end).start())
            drains.append(lambda: self.drain(q))

        def relay(self, q=0):
            @pl.when(inner)
            def _():
                self.copy(q, 0, end, edge).wait_recv()
                self.copy(q, 3, end, edge).start()

        def wait(self, q=0):
            self.copy(q, 0, far, mate).wait_recv()
            self.copy(q, 0, mate, mate).wait_recv()
            pl.when(outer)(lambda: self.copy(q, 0, end, mate).wait_recv())

        def drain(self, q):
            self.copy(q, 0, z, mate).wait_send()
            self.copy(q, 1, z, mate).wait_send()

            @pl.when(inner)
            def _():
                self.copy(q, 2, z, mate).wait_send()
                self.copy(q, 3, z, mate).wait_send()

    par0, own0, par1, own1 = Gather(0, thp, 0, NQ), Gather(1, tho, 0, NQ), Gather(2, thp, 1, 1), Gather(3, tho, 1, 1)

    NB = NQ // 2
    direct = range(NB, NQ)
    shared = range(NB)
    for q in (*direct, *shared):
        cross(0, q, NQ)
    for q in shared:
        own0.start(q)
    for q in direct:
        theta_x(0, q, NQ).wait_recv()
        par0.start(q)
    for q in shared:
        for source in (mate, far):
            own0.copy(q, 0, source, mate).wait_recv()
            cross(0, q, NQ, source)
        own0.relay(q)
        pl.when(inner)(lambda: theta_x(0, q, NQ, end).start())
    for q in direct:
        par0.relay(q)
    for q in shared:

        @pl.when(outer)
        def _():
            own0.copy(q, 0, end, mate).wait_recv()
            theta_x(0, q, NQ, end).start()

        drains.append(theta_x(0, q, NQ, end).wait_send)

    cross(1, 0, 1)
    for q in direct:
        own0.start(q)
    for q in direct:
        par0.wait(q)
    for q in shared:
        for source in (z, mate, far, end):
            theta_x(0, q, NQ, source).wait_recv()

    def a_copy(p, c):
        w, first, rows, n = pieces[p]
        part = (w, pl.ds(c * (G // n), G // n), pl.ds(first, rows))
        return remote(asend.at[part], arecv.at[part], ass.at[p, c], asr.at[p, c], partner)

    def send_amplitudes(p, lo=0, hi=None):
        w, first, rows, n = pieces[p]
        size = G // n

        @pl.loop(lo, n if hi is None else hi)
        def _(c):
            if p == 0:
                c_copy(c).wait()
            part = pl.ds(c * size, size)
            block = jnp.dot(cv[part, pl.ds(first, rows)].reshape(size * rows, M), thp[w], preferred_element_type=F32)
            asend[w, part, pl.ds(first, rows)] = block.astype(BF16).reshape(size, rows, R)
            a_copy(p, c).start()

        def drain():
            @pl.loop(lo, n if hi is None else hi)
            def _(c):
                a_copy(p, c).wait_send()

        drains.append(drain)

    GD = 2 * GC

    def diagonal(w):
        @pl.loop(0, G // GD)
        def _(c):
            part = pl.ds(c * GD, GD)
            block = jnp.dot(cv[part].reshape(GD * R, M), tho[w], preferred_element_type=F32)
            adiag[w, part] = block.astype(BF16).reshape(GD, R, R)

    def accumulate(stream, first, rows, block, part, size):
        lhs = jnp.concatenate([block[g] for g in range(size)], axis=1)
        for n in range(4):
            cols = pl.ds(n * Q, Q)
            acc[stream, pl.ds(first, rows), cols] += jnp.dot(
                lhs, cv[part, :, cols].reshape(size * R, Q), preferred_element_type=F32
            )

    def own_gradient(w):
        @pl.loop(0, G // GD)
        def _(c):
            part = pl.ds(c * GD, GD)
            accumulate(w, 0, R, adiag[w, part], part, GD)

    def swapped_gradient(p, lo=0, hi=None, step=1):
        w, first, rows, n = pieces[p]
        size = step * (G // n)

        @pl.loop(lo // step, (n if hi is None else hi) // step)
        def _(c):
            for k in range(step):
                a_copy(p, c * step + k).wait_recv()
            part = pl.ds(c * size, size)
            accumulate(W + w, first, rows, arecv[w, part, pl.ds(first, rows)], part, size)

    class Scatter:
        def __init__(self, e):
            self.e = e
            self.stream, self.first, self.rows = parts[e]
            self.span = pl.ds(self.first, self.rows)

        def own(self, d):
            return acc[self.stream, self.span, pl.ds(pl.multiple_of(d * Q, Q), Q)]

        def to_mate(self):
            at = (self.stream, 0, self.span)
            return remote(gs.at[at], gr.at[at], gss.at[self.e, 0], gsr.at[self.e, 0], on(mate))

        def to_near(self, k):
            return remote(gs.at[self.stream, 1 + k, self.span], gf.at[self.stream, k, self.span], gss.at[self.e, 1 + k], gsr.at[self.e, 1 + k], on(near))

        def across(self, k, to):
            return remote(gc.at[self.stream, k, self.span], gr.at[self.stream, 1, self.span], gss.at[self.e, 3 + k], gsr.at[self.e, 3], on(to))

        def start(self):
            @pl.when(outer)
            def _():
                for k, d in enumerate((far, end)):
                    gs[self.stream, 1 + k, self.span] = self.own(d).astype(BF16)
                    self.to_near(k).start()

            gs[self.stream, 0, self.span] = self.own(mate).astype(BF16)
            self.to_mate().start()
            drains.append(self.drain)

        def relay(self):
            @pl.when(inner)
            def _():
                for k, d in enumerate((far, end)):
                    self.to_near(k).wait_recv()
                    gc[self.stream, k, self.span] = (self.own(d) + gf[self.stream, k, self.span].astype(F32)).astype(BF16)
                    self.across(k, d).start()

        def total(self):
            self.to_mate().wait_recv()
            self.across(0, far).wait_recv()
            return self.own(z) + gr[self.stream, 0, self.span].astype(F32) + gr[self.stream, 1, self.span].astype(F32)

        def drain(self):
            self.to_mate().wait_send()

            @pl.when(outer)
            def _():
                for k in range(2):
                    self.to_near(k).wait_send()

            @pl.when(inner)
            def _():
                for k in range(2):
                    self.across(k, far).wait_send()

    def x_copy(e):
        stream, first, rows = parts[e]
        at = (stream - W, pl.ds(first, rows))
        return remote(xs.at[at], xr.at[at], xss.at[e], xsr.at[e], partner)

    def finish(e):
        stream, first, rows = parts[e]
        total = scatters[e].total()
        if stream < W:
            gown[stream] = total
        else:
            xs[stream - W, pl.ds(first, rows)] = total.astype(BF16)
            x_copy(e).start()
            drains.append(x_copy(e).wait_send)

    scatters = [Scatter(e) for e in range(len(parts))]
    D0, D1, F0, Fa, Fb, Fc = range(6)

    send_amplitudes(0, 0, 3)
    for q in direct:
        own0.relay(q)
    theta_x(1, 0, 1).wait_recv()
    par1.start()
    send_amplitudes(0, 3, 8)
    for q in direct:
        own0.wait(q)
    diagonal(0)
    par1.relay()
    own1.start()
    own_gradient(0)
    scatters[D0].start()
    swapped_gradient(0, 0, 2, 2)
    par1.wait()
    send_amplitudes(1)
    swapped_gradient(0, 2, 4, 2)
    own1.relay()
    scatters[D0].relay()
    send_amplitudes(2)
    send_amplitudes(3)
    swapped_gradient(0, 4, 8, 2)
    scatters[F0].start()
    own1.wait()
    diagonal(1)
    own_gradient(1)
    scatters[D1].start()
    scatters[F0].relay()
    finish(D0)
    swapped_gradient(1)
    scatters[Fa].start()
    finish(F0)
    scatters[D1].relay()
    swapped_gradient(2)
    scatters[Fb].start()
    scatters[Fa].relay()
    finish(D1)
    swapped_gradient(3)
    scatters[Fc].start()
    scatters[Fb].relay()
    finish(Fa)
    finish(Fb)
    scatters[Fc].relay()
    finish(Fc)
    for e in (F0, Fa, Fb, Fc):
        x_copy(e).wait_recv()

    for w in range(W):
        out[w] = -(gown[w] + xr[w].astype(F32)).T

    for drain in drains:
        drain()


def fused(chol_half, theta):
    G, R, M = chol_half.shape
    W, Q, _ = theta.shape
    CH = 8
    NQ = 4
    H = R // 2
    pieces = ((0, 0, R, CH), (1, 0, H, 4), (1, H, H // 2, 2), (1, H + H // 2, H // 2, 4))
    parts = ((0, 0, R), (1, 0, R), (W, 0, R)) + tuple((W + 1, first, rows) for _, first, rows, _ in pieces[1:])
    dims = (G, R, M, W, Q, CH, NQ, pieces, parts)
    E, PC = len(parts), len(pieces)
    dma = pltpu.SemaphoreType.DMA
    return pl.pallas_call(
        functools.partial(kernel, dims),
        out_shape=jax.ShapeDtypeStruct((W, Q, R), F32),
        in_specs=[pl.BlockSpec(memory_space=pl.ANY), pl.BlockSpec(memory_space=pltpu.VMEM)],
        out_specs=pl.BlockSpec(memory_space=pltpu.VMEM),
        scratch_shapes=[
            pltpu.VMEM((G, R, M), BF16),
            pltpu.VMEM((W, M, R), BF16),
            pltpu.VMEM((W, M, R), BF16),
            pltpu.VMEM((W, G, R, R), BF16),
            pltpu.VMEM((W, G, R, R), BF16),
            pltpu.VMEM((W, G, R, R), BF16),
            pltpu.VMEM((2 * W, R, M), F32),
            pltpu.VMEM((2 * W, 3, R, Q), BF16),
            pltpu.VMEM((2 * W, 2, R, Q), BF16),
            pltpu.VMEM((2 * W, 2, R, Q), BF16),
            pltpu.VMEM((2 * W, 2, R, Q), BF16),
            pltpu.VMEM((W, R, Q), F32),
            pltpu.VMEM((W, R, Q), BF16),
            pltpu.VMEM((W, R, Q), BF16),
            dma((CH,)),
            dma((W, NQ, 4)),
            dma((W, NQ, 4)),
            dma((2 * W, NQ, 4)),
            dma((2 * W, NQ, 4)),
            dma((PC, CH)),
            dma((PC, CH)),
            dma((E, 5)),
            dma((E, 4)),
            dma((E,)),
            dma((E,)),
        ],
        compiler_params=pltpu.CompilerParams(collective_id=0, has_side_effects=True, vmem_limit_bytes=60 << 20),
    )(chol_half, theta)


def on_device(mesh, chol_half, theta):
    G, R, M = chol_half.shape
    nz = mesh.shape["vec"]
    fits = theta.shape[0] == 2 and G % 16 == 0 and R == 128 and theta.shape[1] % 512 == 0 and G * R * M <= 8 << 20
    if mesh.shape["occ"] == 2 and nz == 4 and fits:
        return fused(chol_half, theta)
    widened = lax.all_gather(theta, "occ", axis=2, tiled=True)
    amplitude_sums = jnp.einsum(
        "gip,wpj->wgij", chol_half, lax.all_gather(widened, "vec", axis=1, tiled=True), preferred_element_type=F32
    )
    amplitudes = amplitude_sums.astype(BF16)
    swapped = lax.all_to_all(amplitudes, "occ", split_axis=3, concat_axis=2, tiled=True)
    summed_rows = lax.psum_scatter(
        jnp.einsum("gap,wgba->pwb", chol_half, swapped, preferred_element_type=F32),
        "vec",
        scatter_dimension=0,
        tiled=True,
    )
    owned = lax.psum_scatter(summed_rows, "occ", scatter_dimension=2, tiled=True)
    return -jnp.transpose(owned, (1, 0, 2))


def solution(mesh):
    return jax.shard_map(
        functools.partial(on_device, mesh),
        mesh=mesh,
        in_specs=(P(("grp", "vec"), "occ", None), P(("grp", "wlk"), "vec", "occ")),
        out_specs=P(("grp", "wlk"), "vec", "occ"),
        check_vma=False,
    )
```

time: 107 us -> 86.2 us (0.81)
  the two profiles are of different devices: /device:TPU:24 before, /device:TPU:0 now
where the time goes in v1:
time: 86.2 us; the launch traced here: 86 us
  Pallas kernels  84.1 us (98%)
  local copies, waits for them, and re-layouts  1.87 us (2%)
    pallas_call x1, Pallas kernels, fused(): pl.pallas_call(functools.partial(kernel, dims), out_shape=jax.ShapeDtypeS...  84.1 us
    unnamed x1, local copies, waits for them, and re-layouts  1.87 us

profile of v1, /device:TPU:0, one launch (start us, length us, event | category | flops | bytes accessed | tf_op | source)
XLA Modules:
  0.0 86.0 jit_solution(12843236062892208090)
XLA Ops:
  0.0 84.1 %shard_map.28 = f32[2,512,128]{2,1,0:T(8,128)} custom-call(bf16[32,128,2048]{2,1,0:T(8,128)(2,1)} %chol.1, bf16[2,512,128]{2,1,0:T(8,128)(2,1)} %theta.1), custom_call_target="tpu_custom_call" | custom-call | tf_op jit(solution)/shard_map/pallas_call | solution.py:339
  84.1 1.9 %copy.4 = f32[2,512,128]{2,1,0:T(8,128)} copy(f32[2,512,128]{2,1,0:T(8,128)} %shard_map.28) | data formatting | bytes 1048576

commit v2 on v1

v2 whole, which is shorter than its diff:
```python
import functools

import jax
import jax.numpy as jnp
from jax import lax
from jax.experimental import pallas as pl
from jax.experimental.pallas import tpu as pltpu
from jax.sharding import PartitionSpec as P

MESH = pl.DeviceIdType.MESH
F32 = jnp.float32
BF16 = jnp.bfloat16


def kernel(dims, chol, theta, out, cv, ov, th, asend, arecv, adiag, acc, gs, gf, gc, gr, gown, xs, xr,
           csem, tsem, osem, txs, txr, txq, ags, agq, agr, ass, asr, gss, gsr, xss, xsr):
    G, R, M, W, Q, CH, NQ, NB, pieces, parts = dims
    z = lax.axis_index("vec")
    partner = {"occ": 1 - lax.axis_index("occ")}
    side = z // 2
    near, edge = 1 + side, 3 * side
    far, end = 3 - near, 3 - edge
    core = lax.axis_index("wlk")
    inner = z == near
    outer = z == edge
    mate = near + edge - z
    mine = pl.ds(pl.multiple_of(z * Q, Q), Q)
    GC = G // CH
    QC = Q // NQ

    drains = []

    def remote(src, dst, ss, rs, to):
        return pltpu.make_async_remote_copy(src_ref=src, dst_ref=dst, send_sem=ss, recv_sem=rs, device_id=to, device_id_type=MESH)

    def on(s):
        return {"vec": s}

    def c_copy(c):
        part = pl.ds(c * GC, GC)
        return pltpu.make_async_copy(chol.at[part], cv.at[part], csem)

    OWN, OTHER = pl.ds(0, R), pl.ds(R, R)

    def t_copy(w):
        return pltpu.make_async_copy(theta.at[w], th.at[w, mine, OWN], tsem.at[w])

    for w in range(W):
        t_copy(w).start()

    barrier = pltpu.get_barrier_semaphore()
    greeted = [partner]
    for k in range(1, 4):
        greeted.append(on(lax.rem(z + k, 4)))
    for device in greeted:
        pl.semaphore_signal(barrier, inc=1, device_id=device, device_id_type=MESH)
    acc[...] = jnp.zeros_like(acc)
    pl.semaphore_wait(barrier, len(greeted))

    def rows_of(s, q, n):
        size = Q // n
        return pl.ds(pl.multiple_of(s * Q + q * size, size), size)

    def cross(w, rows):
        remote(th.at[w, rows, OWN], th.at[w, rows, OTHER], txs.at[w], txr.at[w], partner).start()

    def crossed(w, rows):
        rows = pl.ds(0, rows)
        return remote(th.at[w, rows, OWN], th.at[w, rows, OTHER], txs.at[w], txr.at[w], partner)

    def cross_first(q):
        rows = rows_of(z, q, NQ)
        return remote(th.at[0, rows, OWN], th.at[0, rows, OTHER], txs.at[0], txq.at[q], partner)

    class Gather:
        def __init__(self, s, columns, w, n):
            self.s, self.columns, self.w, self.n = s, columns, w, n

        def block(self, rows, recv, to):
            ref = th.at[self.w, rows, self.columns]
            return remote(ref, ref, ags.at[self.s], recv, on(to))

        def recv(self, q, kind):
            return agr.at[self.s, kind // 2] if self.n == 1 else agq.at[self.s - 2, q, kind]

        def copy(self, q, source, to, kind):
            return self.block(rows_of(source, q, self.n), self.recv(q, kind), to)

        def start(self, q=0):
            self.begin(q)
            drains.append(self.drain)

        def begin(self, q=0):
            own = functools.partial(self.copy, q, z)
            own(mate, 0).start()

            @pl.when(inner)
            def _():
                own(far, 1).start()
                own(end, 1).start()

            pl.when(outer)(lambda: own(far, 2).start())

        def arrive(self, q, source, kind):
            self.copy(q, source, mate, kind).wait_recv()

        def relay(self, q=0):
            @pl.when(inner)
            def _():
                self.arrive(q, end, 2)
                self.copy(q, end, edge, 2).start()

        def wait(self, q=0):
            if self.n == 1:
                self.block(pl.ds(0, 2 * Q), self.recv(0, 0), mate).wait_recv()
            else:
                self.arrive(q, mate, 0)
                self.arrive(q, far, 1)
            pl.when(outer)(lambda: self.arrive(q, end, 2))

        def drain(self):
            size = Q // self.n
            pl.when(inner)(lambda: self.block(pl.ds(0, 4 * size), self.recv(0, 0), mate).wait_send())
            pl.when(outer)(lambda: self.block(pl.ds(0, 2 * size), self.recv(0, 0), mate).wait_send())

    own0, par0, own1, par1 = Gather(2, OWN, 0, NQ), Gather(3, OTHER, 0, NQ), Gather(0, OWN, 1, 1), Gather(1, OTHER, 1, 1)
    direct, shared = range(NB, NQ), range(NB)

    t_copy(0).wait()
    for c in range(CH):
        c_copy(c).start()
    for q in direct:
        cross_first(q).start()
    for q in shared:
        own0.start(q)
        cross(0, rows_of(z, q, NQ))
    t_copy(1).wait()
    cross(1, mine)
    drains.append(crossed(0, Q + 3 * NB * (Q // NQ)).wait_send)
    drains.append(crossed(1, Q).wait_send)
    for q in direct:
        cross_first(q).wait_recv()
        par0.start(q)
    for q in shared:
        for kind, source in enumerate((mate, far)):
            own0.arrive(q, source, kind)
            cross(0, rows_of(source, q, NQ))
        own0.relay(q)
        pl.when(inner)(lambda: cross(0, rows_of(end, q, NQ)))
    for q in direct:
        par0.relay(q)
    for q in shared:

        @pl.when(outer)
        def _():
            own0.arrive(q, end, 2)
            cross(0, rows_of(end, q, NQ))

    for q in direct:
        own0.start(q)
    for q in direct:
        par0.wait(q)
    crossed(1, Q).wait_recv()
    par1.start()
    own1.start()
    pltpu.make_async_copy(chol, cv, csem).wait()
    crossed(0, 4 * NB * (Q // NQ)).wait_recv()

    def a_copy(p, c, count=1):
        w, first, rows, n, step = pieces[p]
        part = (w, pl.ds(c * (G // n), count * (G // n)), pl.ds(first, rows))
        return remote(asend.at[part], arecv.at[part], ass.at[p], asr.at[p, c // step], partner)

    def send_amplitudes(p, lo=0, hi=None, both=False):
        w, first, rows, n, step = pieces[p]
        size = G // n
        span = pl.ds(first, rows)

        @pl.loop(lo, n if hi is None else hi)
        def _(c):
            part = pl.ds(c * size, size)
            lhs = cv[part, span].reshape(size * rows, M)
            if both:
                block = jnp.dot(lhs, th[w], preferred_element_type=F32).astype(BF16)
                asend[w, part, span] = block[:, R:].reshape(size, rows, R)
                a_copy(p, c).start()
                adiag[w, part, span] = block[:, :R].reshape(size, rows, R)
            else:
                block = jnp.dot(lhs, th[w, :, OTHER], preferred_element_type=F32).astype(BF16)
                asend[w, part, span] = block.reshape(size, rows, R)
                a_copy(p, c).start()

        if lo == 0:
            drains.append(a_copy(p, 0, n).wait_send)

    GD = 2 * GC

    def diagonal(w, lo, hi):
        @pl.loop(lo, hi)
        def _(c):
            part = pl.ds(c * GD, GD)
            block = jnp.dot(cv[part].reshape(GD * R, M), th[w, :, OWN], preferred_element_type=F32)
            adiag[w, part] = block.astype(BF16).reshape(GD, R, R)

    def accumulate(stream, first, rows, block, part, size):
        lhs = jnp.concatenate([block[g] for g in range(size)], axis=1)
        for n in range(4):
            cols = pl.ds(n * Q, Q)
            acc[stream, pl.ds(first, rows), cols] += jnp.dot(
                lhs, cv[part, :, cols].reshape(size * R, Q), preferred_element_type=F32
            )

    def own_gradient(w):
        @pl.loop(0, G // GD)
        def _(c):
            part = pl.ds(c * GD, GD)
            accumulate(w, 0, R, adiag[w, part], part, GD)

    def swapped_gradient(p, lo=0, hi=None):
        w, first, rows, n, step = pieces[p]
        size = step * (G // n)

        @pl.loop(lo, n // step if hi is None else hi)
        def _(c):
            a_copy(p, c * step, step).wait_recv()
            part = pl.ds(c * size, size)
            accumulate(W + w, first, rows, arecv[w, part, pl.ds(first, rows)], part, size)

    class Scatter:
        def __init__(self, e):
            self.e = e
            self.stream, self.first, self.rows, self.direct = parts[e]
            self.span = pl.ds(self.first, self.rows)

        def own(self, d):
            return acc[self.stream, self.span, pl.ds(pl.multiple_of(d * Q, Q), Q)]

        def link(self, src, dst, k, to):
            return remote(src, dst, gss.at[self.e], gsr.at[self.e, k], on(to))

        def straight(self, k, to, slot=None):
            return self.link(gs.at[self.stream, k, self.span], gr.at[self.stream, k if slot is None else slot, self.span], 0, to)

        def to_near(self, k):
            return self.link(gs.at[self.stream, 1 + k, self.span], gf.at[self.stream, k, self.span], 1 + k, near)

        def across(self, k, to):
            return self.link(gc.at[self.stream, k, self.span], gr.at[self.stream, 1, self.span], 0, to)

        def arrived(self, count):
            return self.link(gs.at[self.stream, pl.ds(0, count), self.span], gr.at[self.stream, pl.ds(0, count), self.span], 0, mate)

        def to_owner(self, d):
            at = (self.stream, d, self.span)
            return remote(gs.at[at], gr.at[self.stream, z, self.span], gss.at[self.e], gsr.at[self.e, 0], {**partner, **on(d)})

        def to_owners(self):
            at = (self.stream, pl.ds(0, 4), self.span)
            return remote(gs.at[at], gr.at[at], gss.at[self.e], gsr.at[self.e, 0], partner)

        def start(self):
            if self.direct == 2:
                for d in range(4):
                    gs[self.stream, d, self.span] = self.own(d).astype(BF16)
                for k in (end, far, near, edge):
                    self.to_owner(k).start()
                drains.append(self.to_owners().wait_send)
                return
            if self.direct:
                for k, d in ((2, 3 - z), (1, 3 - mate), (0, mate)):
                    gs[self.stream, k, self.span] = self.own(d).astype(BF16)
                    self.straight(k, d).start()
            else:

                @pl.when(outer)
                def _():
                    for k, d in enumerate((far, end)):
                        gs[self.stream, 1 + k, self.span] = self.own(d).astype(BF16)
                        self.to_near(k).start()

                gs[self.stream, 0, self.span] = self.own(mate).astype(BF16)
                self.straight(0, mate).start()
            drains.append(self.arrived(3).wait_send)

        def relay(self):
            @pl.when(inner)
            def _():
                for k, d in enumerate((far, end)):
                    self.to_near(k).wait_recv()
                    gc[self.stream, k, self.span] = (self.own(d) + gf[self.stream, k, self.span].astype(F32)).astype(BF16)
                    self.across(k, d).start()

        def total(self):
            count = 3 if self.direct else 2
            self.arrived(count).wait_recv()
            total = self.own(z)
            for k in range(count):
                total += gr[self.stream, k, self.span].astype(F32)
            return total

    def x_copy(w, rows=None):
        if rows is None:
            rows = pl.ds(0, sum(size for stream, _, size, mode in parts if stream == W + w and mode < 2))
        return remote(xs.at[w, rows], xr.at[w, rows], xss.at[w], xsr.at[w], partner)

    def finish(e):
        stream, first, rows, _ = parts[e]
        total = scatters[e].total()
        if stream < W:
            gown[stream] = total
        else:
            w, span = stream - W, pl.ds(first, rows)
            xs[w, span] = total.astype(BF16)
            x_copy(w, span).start()
            if first == 0:
                drains.append(x_copy(w).wait_send)

    def settle(count=None):
        count = len(drains) if count is None else count
        for drain in drains[:count]:
            drain()
        del drains[:count]

    def store(w):
        x_copy(w).wait_recv()
        for e, (stream, first, rows, mode) in enumerate(parts):
            if stream == W + w:
                span = pl.ds(first, rows)
                if mode == 2:
                    scatters[e].to_owners().wait_recv()
                    for d in range(4):
                        gown[w, span] += gr[stream, d, span].astype(F32)
                else:
                    gown[w, span] += xr[w, span].astype(F32)
        ov[w] = -gown[w].T
        pltpu.make_async_copy(ov.at[w], out.at[w], osem).start()
        if w == 0:
            drains.append(pltpu.make_async_copy(ov, out, osem).wait)

    scatters = [Scatter(e) for e in range(len(parts))]
    D0, D1, F0, Fa, Fb, Fc = range(6)

    send_amplitudes(0, 0, 4, both=True)
    par1.relay()
    send_amplitudes(0, 4, 8, both=True)
    own1.relay()
    own_gradient(0)
    scatters[D0].start()
    swapped_gradient(0, 0, 1)
    par1.wait()
    own1.wait()
    send_amplitudes(1, both=True)
    scatters[D0].relay()
    swapped_gradient(0, 1, 2)
    send_amplitudes(2, both=True)
    send_amplitudes(3, both=True)
    own_gradient(1)
    scatters[D1].start()
    swapped_gradient(0, 2, 4)
    scatters[F0].start()
    old = len(drains)
    finish(D0)
    swapped_gradient(1, 0, 1)
    scatters[D1].relay()
    swapped_gradient(1, 1, 4)
    scatters[Fa].start()
    scatters[F0].relay()
    swapped_gradient(2)
    scatters[Fb].start()
    scatters[Fa].relay()
    swapped_gradient(3)
    scatters[Fc].start()
    settle(old)
    finish(D1)
    finish(F0)
    finish(Fa)
    finish(Fb)
    finish(Fc)
    store(0)
    store(1)
    settle()


def fused(chol_half, theta):
    G, R, M = chol_half.shape
    W, Q, _ = theta.shape
    CH = 8
    NQ, NB = 4, 4
    H = R // 4
    modes = (0, 1, 1)
    pieces = ((0, 0, R, CH, 2), (1, 0, 2 * H, 4, 1), (1, 2 * H, H, 4, 1), (1, 3 * H, H, 4, 1))
    parts = ((0, 0, R, 0), (1, 0, R, 0), (W, 0, R, 0)) + tuple(
        (W + 1, first, rows, mode) for (_, first, rows, _, _), mode in zip(pieces[1:], modes)
    )
    dims = (G, R, M, W, Q, CH, NQ, NB, pieces, parts)
    E, PC = len(parts), len(pieces)
    dma = pltpu.SemaphoreType.DMA
    return pl.pallas_call(
        functools.partial(kernel, dims),
        out_shape=jax.ShapeDtypeStruct((W, Q, R), F32),
        in_specs=[pl.BlockSpec(memory_space=pl.ANY)] * 2,
        out_specs=pl.BlockSpec(memory_space=pl.ANY),
        scratch_shapes=[
            pltpu.VMEM((G, R, M), BF16),
            pltpu.VMEM((W, Q, R), F32),
            pltpu.VMEM((W, M, 2 * R), BF16),
            pltpu.VMEM((W, G, R, R), BF16),
            pltpu.VMEM((W, G, R, R), BF16),
            pltpu.VMEM((W, G, R, R), BF16),
            pltpu.VMEM((2 * W, R, M), F32),
            pltpu.VMEM((2 * W, 4, R, Q), BF16),
            pltpu.VMEM((2 * W, 2, R, Q), BF16),
            pltpu.VMEM((2 * W, 2, R, Q), BF16),
            pltpu.VMEM((2 * W, 4, R, Q), BF16),
            pltpu.VMEM((W, R, Q), F32),
            pltpu.VMEM((W, R, Q), BF16),
            pltpu.VMEM((W, R, Q), BF16),
            dma,
            dma((W,)),
            dma,
            dma((W,)),
            dma((W,)),
            dma((NQ,)),
            dma((4,)),
            dma((2, NQ, 3)),
            dma((2, 2)),
            dma((PC,)),
            dma((PC, 4)),
            dma((E,)),
            dma((E, 3)),
            dma((W,)),
            dma((W,)),
        ],
        compiler_params=pltpu.CompilerParams(collective_id=0, has_side_effects=True, vmem_limit_bytes=60 << 20),
    )(chol_half, theta)


def on_device(mesh, chol_half, theta):
    G, R, M = chol_half.shape
    nz = mesh.shape["vec"]
    fits = theta.shape[0] == 2 and G % 16 == 0 and R == 128 and theta.shape[1] % 512 == 0 and G * R * M <= 8 << 20
    if mesh.shape["occ"] == 2 and nz == 4 and fits:
        return fused(chol_half, theta)
    widened = lax.all_gather(theta, "occ", axis=2, tiled=True)
    amplitude_sums = jnp.einsum(
        "gip,wpj->wgij", chol_half, lax.all_gather(widened, "vec", axis=1, tiled=True), preferred_element_type=F32
    )
    amplitudes = amplitude_sums.astype(BF16)
    swapped = lax.all_to_all(amplitudes, "occ", split_axis=3, concat_axis=2, tiled=True)
    summed_rows = lax.psum_scatter(
        jnp.einsum("gap,wgba->pwb", chol_half, swapped, preferred_element_type=F32),
        "vec",
        scatter_dimension=0,
        tiled=True,
    )
    owned = lax.psum_scatter(summed_rows, "occ", scatter_dimension=2, tiled=True)
    return -jnp.transpose(owned, (1, 0, 2))


def solution(mesh):
    return jax.shard_map(
        functools.partial(on_device, mesh),
        mesh=mesh,
        in_specs=(P(("grp", "vec"), "occ", None), P(("grp", "wlk"), "vec", "occ")),
        out_specs=P(("grp", "wlk"), "vec", "occ"),
        check_vma=False,
    )
```

time: 86.2 us -> 78.6 us (0.912)
  Pallas kernels: 84.1 us -> 76.6 us
    pallas_call x1, Pallas kernels: 84.1 us -> 76.6 us  [fused(): pl.pallas_call(functools.partial(kernel, dims), out_shape=jax.ShapeDtypeS...]
where the time goes in v2:
time: 78.6 us; the launch traced here: 78.5 us
  Pallas kernels  76.6 us (97%)
  local copies, waits for them, and re-layouts  1.87 us (2%)
    pallas_call x1, Pallas kernels, fused(): pl.pallas_call(functools.partial(kernel, dims), out_shape=jax.ShapeDtypeS...  76.6 us
    unnamed x1, local copies, waits for them, and re-layouts  1.87 us

profile of v2, /device:TPU:0, one launch (start us, length us, event | category | flops | bytes accessed | tf_op | source)
XLA Modules:
  0.0 78.5 jit_solution(15199861895242410712)
XLA Ops:
  0.0 76.6 %shard_map.28 = f32[2,512,128]{2,1,0:T(8,128)} custom-call(bf16[32,128,2048]{2,1,0:T(8,128)(2,1)} %chol.1, bf16[2,512,128]{2,1,0:T(8,128)(2,1)} %theta.1), custom_call_target="tpu_custom_call" | custom-call | tf_op jit(solution)/shard_map/pallas_call | solution.py:398
  76.6 1.9 %copy.4 = f32[2,512,128]{2,1,0:T(8,128)} copy(f32[2,512,128]{2,1,0:T(8,128)} %shard_map.28) | data formatting | bytes 1048576

commit v3 on v2

--- a/solution.py
+++ b/solution.py
@@ -12,8 +12,8 @@
 BF16 = jnp.bfloat16
 
 
-def kernel(dims, chol, theta, out, cv, ov, th, asend, arecv, adiag, acc, gs, gf, gc, gr, gown, xs, xr,
-           csem, tsem, osem, txs, txr, txq, ags, agq, agr, ass, asr, gss, gsr, xss, xsr):
+def kernel(dims, chol, theta, out, cv, th, asend, arecv, adiag, acc, gs, gf, gc, gr, gown, xs, xr,
+           csem, tsem, txs, txr, txq, ags, agq, agr, ass, asr, gss, gsr, xss, xsr):
     G, R, M, W, Q, CH, NQ, NB, pieces, parts = dims
     z = lax.axis_index("vec")
     partner = {"occ": 1 - lax.axis_index("occ")}
@@ -54,7 +54,6 @@
         greeted.append(on(lax.rem(z + k, 4)))
     for device in greeted:
         pl.semaphore_signal(barrier, inc=1, device_id=device, device_id_type=MESH)
-    acc[...] = jnp.zeros_like(acc)
     pl.semaphore_wait(barrier, len(greeted))
 
     def rows_of(s, q, n):
@@ -134,6 +133,7 @@
     for q in shared:
         own0.start(q)
         cross(0, rows_of(z, q, NQ))
+    acc[...] = jnp.zeros_like(acc)
     t_copy(1).wait()
     cross(1, mine)
     drains.append(crossed(0, Q + 3 * NB * (Q // NQ)).wait_send)
@@ -160,9 +160,6 @@
         own0.start(q)
     for q in direct:
         par0.wait(q)
-    crossed(1, Q).wait_recv()
-    par1.start()
-    own1.start()
     pltpu.make_async_copy(chol, cv, csem).wait()
     crossed(0, 4 * NB * (Q // NQ)).wait_recv()
 
@@ -171,36 +168,40 @@
         part = (w, pl.ds(c * (G // n), count * (G // n)), pl.ds(first, rows))
         return remote(asend.at[part], arecv.at[part], ass.at[p], asr.at[p, c // step], partner)
 
-    def send_amplitudes(p, lo=0, hi=None, both=False):
+    def send_amplitudes(p, lo=0, hi=None, both=False, wide=1):
         w, first, rows, n, step = pieces[p]
-        size = G // n
+        size = wide * (G // n)
         span = pl.ds(first, rows)
 
-        @pl.loop(lo, n if hi is None else hi)
+        @pl.loop(lo // wide, (n if hi is None else hi) // wide)
         def _(c):
             part = pl.ds(c * size, size)
             lhs = cv[part, span].reshape(size * rows, M)
             if both:
                 block = jnp.dot(lhs, th[w], preferred_element_type=F32).astype(BF16)
                 asend[w, part, span] = block[:, R:].reshape(size, rows, R)
-                a_copy(p, c).start()
-                adiag[w, part, span] = block[:, :R].reshape(size, rows, R)
             else:
                 block = jnp.dot(lhs, th[w, :, OTHER], preferred_element_type=F32).astype(BF16)
                 asend[w, part, span] = block.reshape(size, rows, R)
-                a_copy(p, c).start()
+            for k in range(wide):
+                a_copy(p, c * wide + k).start()
+            if both:
+                adiag[w, part, span] = block[:, :R].reshape(size, rows, R)
 
         if lo == 0:
             drains.append(a_copy(p, 0, n).wait_send)
 
     GD = 2 * GC
 
-    def diagonal(w, lo, hi):
-        @pl.loop(lo, hi)
+    def diagonal(w, first, rows):
+        size = min(G, GD * R // rows)
+        span = pl.ds(first, rows)
+
+        @pl.loop(0, G // size)
         def _(c):
-            part = pl.ds(c * GD, GD)
-            block = jnp.dot(cv[part].reshape(GD * R, M), th[w, :, OWN], preferred_element_type=F32)
-            adiag[w, part] = block.astype(BF16).reshape(GD, R, R)
+            part = pl.ds(c * size, size)
+            block = jnp.dot(cv[part, span].reshape(size * rows, M), th[w, :, OWN], preferred_element_type=F32)
+            adiag[w, part, span] = block.astype(BF16).reshape(size, rows, R)
 
     def accumulate(stream, first, rows, block, part, size):
         lhs = jnp.concatenate([block[g] for g in range(size)], axis=1)
@@ -332,47 +333,57 @@
                         gown[w, span] += gr[stream, d, span].astype(F32)
                 else:
                     gown[w, span] += xr[w, span].astype(F32)
-        ov[w] = -gown[w].T
-        pltpu.make_async_copy(ov.at[w], out.at[w], osem).start()
-        if w == 0:
-            drains.append(pltpu.make_async_copy(ov, out, osem).wait)
+        out[w] = -gown[w].T
 
     scatters = [Scatter(e) for e in range(len(parts))]
-    D0, D1, F0, Fa, Fb, Fc = range(6)
-
-    send_amplitudes(0, 0, 4, both=True)
+    D0, D1, F0, G0, Fa, Fb, Fc = range(7)
+
+    send_amplitudes(0, 0, 4, wide=2)
+    for q in direct:
+        own0.relay(q)
+    crossed(1, Q).wait_recv()
+    par1.start()
+    own1.start()
+    send_amplitudes(0, 4, 8, wide=2)
+    for q in direct:
+        own0.wait(q)
+    send_amplitudes(1, both=True, wide=2)
     par1.relay()
-    send_amplitudes(0, 4, 8, both=True)
+    diagonal(0, 0, R // 2)
     own1.relay()
     own_gradient(0)
     scatters[D0].start()
-    swapped_gradient(0, 0, 1)
+    swapped_gradient(0)
+    scatters[F0].start()
     par1.wait()
     own1.wait()
-    send_amplitudes(1, both=True)
+    send_amplitudes(2, both=True, wide=2)
     scatters[D0].relay()
-    swapped_gradient(0, 1, 2)
-    send_amplitudes(2, both=True)
-    send_amplitudes(3, both=True)
+    send_amplitudes(3, both=True, wide=2)
+    send_amplitudes(4, both=True, wide=2)
+    scatters[F0].relay()
     own_gradient(1)
     scatters[D1].start()
-    swapped_gradient(0, 2, 4)
-    scatters[F0].start()
+    swapped_gradient(1)
+    scatters[G0].start()
     old = len(drains)
     finish(D0)
-    swapped_gradient(1, 0, 1)
+    swapped_gradient(2, 0, 2)
     scatters[D1].relay()
-    swapped_gradient(1, 1, 4)
+    swapped_gradient(2, 2, 4)
     scatters[Fa].start()
-    scatters[F0].relay()
-    swapped_gradient(2)
+    swapped_gradient(3, 0, 2)
+    scatters[G0].relay()
+    swapped_gradient(3, 2, 4)
     scatters[Fb].start()
+    swapped_gradient(4, 0, 2)
     scatters[Fa].relay()
-    swapped_gradient(3)
+    swapped_gradient(4, 2, 4)
     scatters[Fc].start()
     settle(old)
+    finish(F0)
+    finish(G0)
     finish(D1)
-    finish(F0)
     finish(Fa)
     finish(Fb)
     finish(Fc)
@@ -385,12 +396,12 @@
     G, R, M = chol_half.shape
     W, Q, _ = theta.shape
     CH = 8
-    NQ, NB = 4, 4
+    NQ, NB = 4, 2
     H = R // 4
-    modes = (0, 1, 1)
-    pieces = ((0, 0, R, CH, 2), (1, 0, 2 * H, 4, 1), (1, 2 * H, H, 4, 1), (1, 3 * H, H, 4, 1))
-    parts = ((0, 0, R, 0), (1, 0, R, 0), (W, 0, R, 0)) + tuple(
-        (W + 1, first, rows, mode) for (_, first, rows, _, _), mode in zip(pieces[1:], modes)
+    modes = (0, 0, 0, 1, 1)
+    pieces = ((0, 0, 2 * H, CH, 2), (0, 2 * H, 2 * H, CH, 2), (1, 0, 2 * H, 4, 1), (1, 2 * H, H, 4, 1), (1, 3 * H, H, 4, 1))
+    parts = ((0, 0, R, 0), (1, 0, R, 0)) + tuple(
+        (W + w, first, rows, mode) for (w, first, rows, _, _), mode in zip(pieces, modes)
     )
     dims = (G, R, M, W, Q, CH, NQ, NB, pieces, parts)
     E, PC = len(parts), len(pieces)
@@ -399,10 +410,9 @@
         functools.partial(kernel, dims),
         out_shape=jax.ShapeDtypeStruct((W, Q, R), F32),
         in_specs=[pl.BlockSpec(memory_space=pl.ANY)] * 2,
-        out_specs=pl.BlockSpec(memory_space=pl.ANY),
+        out_specs=pl.BlockSpec(memory_space=pltpu.VMEM),
         scratch_shapes=[
             pltpu.VMEM((G, R, M), BF16),
-            pltpu.VMEM((W, Q, R), F32),
             pltpu.VMEM((W, M, 2 * R), BF16),
             pltpu.VMEM((W, G, R, R), BF16),
             pltpu.VMEM((W, G, R, R), BF16),
@@ -417,7 +427,6 @@
             pltpu.VMEM((W, R, Q), BF16),
             dma,
             dma((W,)),
-            dma,
             dma((W,)),
             dma((W,)),
             dma((NQ,)),
@@ -431,7 +440,7 @@
             dma((W,)),
             dma((W,)),
         ],
-        compiler_params=pltpu.CompilerParams(collective_id=0, has_side_effects=True, vmem_limit_bytes=60 << 20),
+        compiler_params=pltpu.CompilerParams(collective_id=0, has_side_effects=True, vmem_limit_bytes=50000 << 10),
     )(chol_half, theta)
 
 

time: 78.6 us -> 76.4 us (0.972)
  Pallas kernels: 76.6 us -> 74.5 us
    pallas_call x1, Pallas kernels: 76.6 us -> 74.5 us  [fused(): pl.pallas_call(functools.partial(kernel, dims), out_shape=jax.ShapeDtypeS...]
    unnamed x1 -> x3, local copies, waits for them, and re-layouts: 1.87 us -> 1.75 us
where the time goes in v3:
time: 76.4 us; the launch traced here: 76.3 us
  Pallas kernels  74.5 us (98%)
  local copies, waits for them, and re-layouts  1.75 us (2%)
    pallas_call x1, Pallas kernels, fused(): pl.pallas_call(functools.partial(kernel, dims), out_shape=jax.ShapeDtypeS...  74.5 us
    unnamed x3, local copies, waits for them, and re-layouts  1.75 us

profile of v3, /device:TPU:0, one launch (start us, length us, event | category | flops | bytes accessed | tf_op | source)
XLA Modules:
  0.0 76.3 jit_solution(12952374970398330568)
XLA Ops:
  0.0 0.0 copy-start
  0.0 0.9 %copy-done = bf16[2,512,128]{2,1,0:T(8,128)(2,1)S(1)} copy-done((bf16[2,512,128]{2,1,0:T(8,128)(2,1)S(1)}, bf16[2,512,128]{2,1,0:T(8,128)(2,1)}, u32[]{:S(2)}) %copy-start) | copy-done | bytes 262168
  1.0 74.5 %shard_map.28 = f32[2,512,128]{2,1,0:T(8,128)S(1)} custom-call(bf16[32,128,2048]{2,1,0:T(8,128)(2,1)} %chol.1, bf16[2,512,128]{2,1,0:T(8,128)(2,1)S(1)} %copy-done), custom_call_target="tpu_custom_call" | custom-call | tf_op jit(solution)/shard_map/pallas_call | solution.py:409
  75.5 0.8 %copy.4 = f32[2,512,128]{2,1,0:T(8,128)} copy(f32[2,512,128]{2,1,0:T(8,128)S(1)} %shard_map.28) | data formatting | bytes 1048576
Async XLA Ops:
  0.0 0.9 %copy-start = (bf16[2,512,128]{2,1,0:T(8,128)(2,1)S(1)}, bf16[2,512,128]{2,1,0:T(8,128)(2,1)}, u32[]{:S(2)}) copy-start(bf16[2,512,128]{2,1,0:T(8,128)(2,1)} %theta.1) | copy-start | bytes 786436

commit v4 on v3

--- a/solution.py
+++ b/solution.py
@@ -396,7 +396,7 @@
     G, R, M = chol_half.shape
     W, Q, _ = theta.shape
     CH = 8
-    NQ, NB = 4, 2
+    NQ, NB = 8, 4
     H = R // 4
     modes = (0, 0, 0, 1, 1)
     pieces = ((0, 0, 2 * H, CH, 2), (0, 2 * H, 2 * H, CH, 2), (1, 0, 2 * H, 4, 1), (1, 2 * H, H, 4, 1), (1, 3 * H, H, 4, 1))

time: 76.4 us -> 75.8 us (level)
  no operation moved by 1% of the time
where the time goes in v4:
time: 75.8 us; the launch traced here: 75.6 us
  Pallas kernels  73.9 us (97%)
  local copies, waits for them, and re-layouts  1.75 us (2%)
    pallas_call x1, Pallas kernels, fused(): pl.pallas_call(functools.partial(kernel, dims), out_shape=jax.ShapeDtypeS...  73.9 us
    unnamed x3, local copies, waits for them, and re-layouts  1.75 us

profile of v4, /device:TPU:0, one launch (start us, length us, event | category | flops | bytes accessed | tf_op | source)
XLA Modules:
  0.0 75.6 jit_solution(18442889714641719042)
XLA Ops:
  0.0 0.0 copy-start
  0.0 0.9 %copy-done = bf16[2,512,128]{2,1,0:T(8,128)(2,1)S(1)} copy-done((bf16[2,512,128]{2,1,0:T(8,128)(2,1)S(1)}, bf16[2,512,128]{2,1,0:T(8,128)(2,1)}, u32[]{:S(2)}) %copy-start) | copy-done | bytes 262168
  1.0 73.9 %shard_map.28 = f32[2,512,128]{2,1,0:T(8,128)S(1)} custom-call(bf16[32,128,2048]{2,1,0:T(8,128)(2,1)} %chol.1, bf16[2,512,128]{2,1,0:T(8,128)(2,1)S(1)} %copy-done), custom_call_target="tpu_custom_call" | custom-call | tf_op jit(solution)/shard_map/pallas_call | solution.py:409
  74.8 0.8 %copy.4 = f32[2,512,128]{2,1,0:T(8,128)} copy(f32[2,512,128]{2,1,0:T(8,128)S(1)} %shard_map.28) | data formatting | bytes 1048576
Async XLA Ops:
  0.0 0.9 %copy-start = (bf16[2,512,128]{2,1,0:T(8,128)(2,1)S(1)}, bf16[2,512,128]{2,1,0:T(8,128)(2,1)}, u32[]{:S(2)}) copy-start(bf16[2,512,128]{2,1,0:T(8,128)(2,1)} %theta.1) | copy-start | bytes 786436
